TPU v7x, 32 devices: a whole 2x2x4 slice. The times are simulated.
32 devices in a mesh: dp: 2 (over x), ep: 4 (over z), tp: 4 (over y, core).
Axes of the slice: x: 2, y: 2, z: 4, core: 2. Of those that a mesh axis runs over, the one named last changes fastest.
Arguments:
- X: bfloat16 [4096, 2048], P(('dp', 'ep', 'tp')), parts along dimension 0
- idx: int32 [4096, 8], P(('dp', 'ep', 'tp')), parts along dimension 0
- g: float32 [4096, 8], P(('dp', 'ep', 'tp')), parts along dimension 0
- W1: bfloat16 [64, 2048, 1024], P('ep', None, 'tp')
- W3: bfloat16 [64, 2048, 1024], P('ep', None, 'tp')
- W2: bfloat16 [64, 1024, 2048], P('ep', 'tp')
Outputs:
- output: bfloat16 [4096, 2048], P(('dp', 'ep', 'tp')), parts along dimension 0
There are 2 independent parts. A program takes and returns all parts, laid end to end along the dimension named above; an argument that names none is the same for every part.
All inputs are finite; a program needn't handle non-finite values.
Results may differ from a plain program's by a relative error of at most 0.0102053.
Values are sent between devices in bfloat16 or wider.
A program may use at most 1 GiB of HBM per device.

v0:
```python
import jax
import jax.numpy as jnp
from jax import lax
from jax.sharding import PartitionSpec as P

CF = 2


def _route(idx, n_exp, cap):
    ids = idx.reshape(-1)
    oh = (ids[:, None] == jnp.arange(n_exp, dtype=jnp.int32)[None, :]).astype(jnp.int32)
    s = jnp.sum(oh * (jnp.cumsum(oh, axis=0) - 1), axis=1)
    keep = s < cap
    return jnp.where(keep, ids * cap + s, n_exp * cap), keep


def solution(mesh):
    ep, tp = mesh.shape["ep"], mesh.shape["tp"]
    rows = P(("dp", "ep", "tp"), None)

    def local(x, idx, g, w1, w3, w2):
        t_loc, d = x.shape
        top = idx.shape[1]
        el = w1.shape[0]
        n_exp = el * ep
        cap = CF * top * t_loc // n_exp
        dest, keep = _route(idx, n_exp, cap)
        xr = jnp.repeat(x, top, axis=0)
        buf = jnp.zeros((n_exp * cap, d), x.dtype).at[dest].set(xr, mode="drop").reshape(ep, el, cap, d)
        recv = lax.all_to_all(buf, "ep", 0, 0, tiled=True)
        allr = lax.all_gather(recv, "tp", axis=0)
        xe = allr.transpose(2, 0, 1, 3, 4).reshape(el, tp * ep * cap, d)
        h1 = jnp.einsum("erd,edf->erf", xe, w1, preferred_element_type=jnp.float32)
        h3 = jnp.einsum("erd,edf->erf", xe, w3, preferred_element_type=jnp.float32)
        h = (jax.nn.silu(h1) * h3).astype(jnp.bfloat16)
        yp = jnp.einsum("erf,efd->erd", h, w2, preferred_element_type=jnp.float32).astype(jnp.bfloat16)
        yp = yp.reshape(el, tp, ep, cap, d).transpose(1, 2, 0, 3, 4)
        parts = lax.all_to_all(yp, "tp", 0, 0, tiled=True)
        y = jnp.sum(parts.astype(jnp.float32), axis=0).astype(jnp.bfloat16)
        back = lax.all_to_all(y, "ep", 0, 0, tiled=True).reshape(n_exp * cap, d)
        ysel = back[jnp.minimum(dest, n_exp * cap - 1)].astype(jnp.float32).reshape(t_loc, top, d)
        wgt = jnp.where(keep, g.reshape(-1), 0.0).reshape(t_loc, top, 1)
        return jnp.sum(ysel * wgt, axis=1).astype(jnp.bfloat16)

    return jax.shard_map(local, mesh=mesh,
                         in_specs=(rows, rows, rows, P("ep", None, "tp"), P("ep", None, "tp"), P("ep", "tp", None)),
                         out_specs=rows, check_vma=False)
```

profile of v0, /device:TPU:0, one launch (start us, length us, event | category | flops | bytes accessed | tf_op | source)
XLA Modules:
  0.0 1167.9 jit_solution(11208521087393424443)
XLA Ops:
  6.5 0.8 copy.25
  7.6 0.7 broadcast_multiply_fusion
  8.3 18.0 %reduce-window.6 = s32[64,8,128]{2,1,0:T(8,128)S(1)} reduce-window(s32[64,8,128]{2,1,0:T(8,128)S(1)} %fusion.10, s32[]{:T(128)} %constant.9.clone.1), window={size=1x1x128 pad=0_0x0_0x127_0}, to_apply=%region_0.0 | reduce-window | flops 8323072 | bytes 524292 | tf_op jit(solution)/shard_map/reduce-window
  26.3 0.1 slice.10
  26.4 0.1 copy.27
  26.7 0.1 add_add_fusion
  26.8 0.1 copy.29
  27.1 0.6 copy-done.2
  27.7 0.6 compare_select_fusion
  28.3 11.2 scatter_custom_fusion
  39.6 192.1 %all_to_all.15 = bf16[4,16,32,2048]{3,2,1,0:T(8,128)(2,1)} all-to-all(bf16[4,16,32,2048]{3,2,1,0:T(8,128)(2,1)} %bitcast.51), channel_id=1, replica_groups=mesh['dp'=2,'ep'=4,'tp'=4] {'ep'}, dimensions={0} | all-to-all | bytes 16777216 | tf_op jit(solution)/shard_map/all_to_all | solution.py:30
  231.7 201.3 %all-gather.3.cloned.1.call-done = bf16[16,16,32,2048]{3,2,1,0:T(8,128)(2,1)} async-done(((bf16[4,16,32,2048]{3,2,1,0:T(8,128)(2,1)}), bf16[16,16,32,2048]{3,2,1,0:T(8,128)(2,1)}) %all-gather.3.cloned.1.call-update) | async-done | bytes 33554448 | tf_op jit(solution)/shard_map/all_gather | solution.py:31
  433.0 22.9 %copy.30 = bf16[4,4,16,32,2048]{4,3,1,0,2:T(8,128)(2,1)} copy(bf16[4,4,16,32,2048]{4,3,2,1,0:T(8,128)(2,1)} %bitcast.48) | data formatting | bytes 67108864 | tf_op jit(solution)/shard_map/all_gather | solution.py:31
  455.9 22.9 %fusion.12 = f32[16,512,256]{2,1,0:T(8,128)} fusion(bf16[16,512,2048]{2,1,0:T(8,128)(2,1)} %bitcast.49, bf16[16,2048,256]{2,1,0:T(8,128)(2,1)} %param.9), kind=kOutput, calls=%fused_computation.28 | convolution fusion | flops 8589934592 | bytes 58720256 | tf_op jit(solution)/shard_map/erd,edf->erf/dot_general | solution.py:33
  478.8 23.7 %multiply_convert_fusion.4 = bf16[16,512,256]{2,1,0:T(8,128)(2,1)} fusion(f32[16,512,256]{2,1,0:T(8,128)} %fusion.12, bf16[16,512,2048]{2,1,0:T(8,128)(2,1)} %bitcast.50, bf16[16,2048,256]{2,1,0:T(8,128)(2,1)} %param.10), kind=kOutput, calls=%fused_computation.6.clone.clone.1 | convolution fusion | flops 8602517504 | bytes 62914560 | tf_op jit(solution)/shard_map/erd,edf->erf/dot_general | solution.py:34
  502.5 21.2 %convolution_convert_fusion = bf16[16,512,2048]{2,1,0:T(8,128)(2,1)} fusion(bf16[16,256,2048]{2,1,0:T(8,128)(2,1)} %param.11, bf16[16,512,256]{2,1,0:T(8,128)(2,1)} %multiply_convert_fusion.4), kind=kOutput, calls=%fused_computation.3 | convolution fusion | flops 8606711808 | bytes 54525952 | tf_op jit(solution)/shard_map/erf,efd->erd/dot_general | solution.py:36
  523.7 23.0 %copy.39 = bf16[16,4,4,32,2048]{4,3,2,0,1:T(8,128)(2,1)} copy(bf16[16,4,4,32,2048]{4,3,2,1,0:T(8,128)(2,1)} %bitcast.46) | data formatting | bytes 67108864 | tf_op jit(solution)/shard_map/reshape | solution.py:37
  546.7 380.6 %all_to_all.16 = bf16[4,4,16,32,2048]{4,3,1,2,0:T(8,128)(2,1)} all-to-all(bf16[4,4,16,32,2048]{4,3,1,2,0:T(8,128)(2,1)} %bitcast.47), channel_id=1, replica_groups=mesh['dp'=2,'ep'=4,'tp'=4] {'tp'}, dimensions={0} | all-to-all | bytes 67108864 | tf_op jit(solution)/shard_map/all_to_all | solution.py:38
  927.3 16.4 %reduce_sum.34 = bf16[4,16,32,2048]{3,2,0,1:T(8,128)(2,1)} reduce(bf16[4,4,16,32,2048]{4,3,1,2,0:T(8,128)(2,1)} %all_to_all.16, bf16[]{:T(256)} %constant.8.clone.1), dimensions={0}, to_apply=%region_4.5 | reduce | flops 12582912 | bytes 41943040 | tf_op jit(solution)/shard_map/reduce_sum | solution.py:39
  943.7 8.3 copy.33
  952.0 5.8 all-to-all-start.2
  958.0 182.3 %all-to-all-done.2 = bf16[4,16,32,2048]{3,2,1,0:T(8,128)(2,1)} async-done(((bf16[4,16,32,2048]{3,2,1,0:T(8,128)(2,1)}), bf16[4,16,32,2048]{3,2,1,0:T(8,128)(2,1)}, u32[]{:S(2)}, u32[]{:S(2)}) %all-to-all-start.2) | async-done | bytes 8388640 | tf_op jit(solution)/shard_map/all_to_all | solution.py:40
  1140.3 13.3 %gather_fusion = bf16[1024,2048]{1,0:T(8,128)(2,1)} fusion(bf16[2048,2048]{1,0:T(8,128)(2,1)} %bitcast.12, s32[1024]{0:T(1024)S(1)} %broadcast_clamp_fusion), kind=kCustom, calls=%fused_computation | custom fusion | bytes 8392704 | tf_op jit(solution)/shard_map/gather | solution.py:41
  1153.7 7.3 fusion
  (27 shorter events, 0.7 us)
Async XLA Ops:
  6.5 21.8 %copy-start = (bf16[128,2048]{1,0:T(8,128)(2,1)S(1)}, bf16[128,2048]{1,0:T(8,128)(2,1)}, u32[]{:S(2)}) copy-start(bf16[128,2048]{1,0:T(8,128)(2,1)} %param.6) | copy-start | bytes 1572868
  6.5 426.4 %all-gather.3.cloned.1.call-start = ((), (), s32[]{:S(2)}) async-start(), calls=%async_computation.3 | async-start | bytes 41943040 | tf_op jit(solution)/shard_map/all_gather | solution.py:31
  27.1 0.6 copy-start.2
  952.0 5.8 copy-start.3
  952.0 5.9 copy-start.5
  952.0 6.0 copy-start.4
  952.0 188.4 %all-to-all-start.2 = ((bf16[4,16,32,2048]{3,2,1,0:T(8,128)(2,1)}), bf16[4,16,32,2048]{3,2,1,0:T(8,128)(2,1)}, u32[]{:S(2)}, u32[]{:S(2)}) async-start(bf16[4,16,32,2048]{3,2,1,0:T(8,128)(2,1)} %copy.33), calls=%async_computation.2 | async-start | bytes 16777216 | tf_op jit(solution)/shard_map/all_to_all | solution.py:40
  1140.3 20.7 %copy-start.1 = (bf16[128,2048]{1,0:T(8,128)(2,1)S(1)}, bf16[128,2048]{1,0:T(8,128)(2,1)}, u32[]{:S(2)}) copy-start(bf16[128,2048]{1,0:T(8,128)(2,1)} %param.6) | copy-start | bytes 1572868
Sparse Core Ops, SparseCore 0:
  231.8 201.1 all-gather.2
where the time goes:
time: 1170 us
  blocking collectives  573 us (49%)
  waiting for transfers between devices  384 us (33%)
  local copies, waits for them, and re-layouts  81.1 us (7%)
  matrix products  67.9 us (6%)
  other arithmetic  43.3 us (4%)
  between operations  13.5 us (1%)
    all_to_all x1, blocking collectives, local(): parts = lax.all_to_all(yp, 'tp', 0, 0, tiled=True)  381 us
    all_gather x1, waiting for transfers between devices, local(): allr = lax.all_gather(recv, 'tp', axis=0)  201 us
    all_to_all x1, blocking collectives, local(): recv = lax.all_to_all(buf, 'ep', 0, 0, tiled=True)  192 us
    all_to_all x1, waiting for transfers between devices, local(): back = lax.all_to_all(y, 'ep', 0, 0, tiled=True).reshape(n_exp * cap, d)  182 us
    dot_general x1, matrix products, local(): h3 = jnp.einsum('erd,edf->erf', xe, w3, preferred_element_type=jnp.float32)  23.7 us
  transfers between devices with their start and end apart: 2, of which 2 were waited for; matrix products, arithmetic and copies ran while one was open for 0% of the time, Pallas kernels for 0%

commit v1 on v0

v1 whole, which is shorter than its diff:
```python
import functools

import jax
import jax.numpy as jnp
from jax import lax
from jax.experimental import pallas as pl
from jax.experimental.pallas import tpu as pltpu
from jax.sharding import PartitionSpec as P

MESH = pl.DeviceIdType.MESH
F32 = jnp.float32
BF16 = jnp.bfloat16

T = 128
HALF = T // 2
TOP = 8
EL = 16
CAP = 32
UNITS = 8
ROWS = UNITS * CAP
NS = 4


def _z_order(z, i):
    inner = (z + 1) // 2 - 2 * (z // 3)
    v = (1 - inner) * (1 + i) + inner * (i + (i + 1) // 2)
    m = z // 2
    return m * (3 - v) + (1 - m) * v


def _r_order(z, i):
    inner = (z + 1) // 2 - 2 * (z // 3)
    odd = i % 2
    v = (1 - inner) * (3 - i) + inner * ((1 - odd) * (3 - i // 2) + odd * (i // 2))
    m = z // 2
    return m * (3 - v) + (1 - m) * v


def _kernel(x_ref, aux_ref, w1_ref, w3_ref, w2_ref, out_ref,
            xall, auxall, xe, w1b, w3b, w2b, spread, tab, pown, dstage, drecv, ystage, yrecv, zstage, zrecv,
            fstage, frecv,
            lsem, lasem, dsem, dasem, ssem, sasem, wsem, rd_s, rd_r, ry_s, ry_r, rz_s, rz_r, rf_s, rf_r):
    d = x_ref.shape[1]
    z = lax.axis_index("ep")
    tp = lax.axis_index("tp")
    y = tp // 2
    c = tp % 2
    me = z * 2 + y
    row0 = pl.multiple_of(c * HALF, HALF)
    oth0 = pl.multiple_of((1 - c) * HALF, HALF)
    mine = pl.ds(row0, HALF)
    amine = pl.ds(pl.multiple_of(c * 8, 8), 8)
    up, down = {"ep": z + 1}, {"ep": z - 1}
    ynbr = {"tp": (1 - y) * 2 + c}
    partner = {"tp": y * 2 + (1 - c)}

    def rcopy(src, dst, s, r, dev):
        return pltpu.make_async_remote_copy(src_ref=src, dst_ref=dst, send_sem=s, recv_sem=r,
                                            device_id=dev, device_id_type=MESH)

    def wcopies(q):
        e, s = q % EL, q % NS
        return (pltpu.make_async_copy(w1_ref.at[e], w1b.at[s], wsem.at[s, 0]),
                pltpu.make_async_copy(w3_ref.at[e], w3b.at[s], wsem.at[s, 1]),
                pltpu.make_async_copy(w2_ref.at[e], w2b.at[s], wsem.at[s, 2]))

    for q in range(NS):
        for cp in wcopies(q):
            cp.start()

    bar = pltpu.get_barrier_semaphore()

    @pl.when(z < 3)
    def _():
        pl.semaphore_signal(bar, inc=1, device_id=up, device_id_type=MESH)

    @pl.when(z > 0)
    def _():
        pl.semaphore_signal(bar, inc=1, device_id=down, device_id_type=MESH)

    pl.semaphore_signal(bar, inc=1, device_id=ynbr, device_id_type=MESH)
    pl.semaphore_signal(bar, inc=1, device_id=partner, device_id_type=MESH)
    inner = (z + 1) // 2 - 2 * (z // 3)
    pl.semaphore_wait(bar, 3 + inner)

    def link_send(h, u, xs, xas, k, dev, op):
        cx = rcopy(xs, xall.at[h, u, mine], ssem.at[h, u, k], lsem.at[h, u], dev)
        ca = rcopy(xas, auxall.at[h, u, amine], sasem.at[h, u, k], lasem.at[h, u], dev)
        if op == "start":
            ca.start()
            cx.start()
        else:
            ca.wait_send()
            cx.wait_send()

    def d2d_send(h, u, op):
        cx = rcopy(xall.at[h, u, mine], xall.at[h, u, mine], ssem.at[h, u, 3], dsem.at[h, u], partner)
        ca = rcopy(auxall.at[h, u, amine], auxall.at[h, u, amine], sasem.at[h, u, 3], dasem.at[h, u], partner)
        if op == "start":
            ca.start()
            cx.start()
        else:
            ca.wait_send()
            cx.wait_send()

    def own_full(h, op):
        cx = rcopy(x_ref, xall.at[h, me], ssem.at[h, me, 3], dsem.at[h, me], partner)
        ca = rcopy(aux_ref, auxall.at[h, me], sasem.at[h, me, 3], dasem.at[h, me], partner)
        if op == "start":
            ca.start()
            cx.start()
        elif op == "send":
            ca.wait_send()
            cx.wait_send()
        else:
            ca.wait_recv()
            cx.wait_recv()

    def own_links(h, xs, xas, op):
        @pl.when(z < 3)
        def _():
            link_send(h, me, xs, xas, 0, up, op)

        @pl.when(z > 0)
        def _():
            link_send(h, me, xs, xas, 1, down, op)

        link_send(h, me, xs, xas, 2, ynbr, op)

    def own_start(h):
        @pl.when(c == h)
        def _():
            own_links(h, x_ref.at[mine], aux_ref.at[amine], "start")
            xall[h, me] = x_ref[...]
            auxall[h, me] = aux_ref[...]

        @pl.when(c != h)
        def _():
            own_full(h, "recv")
            own_links(h, xall.at[h, me, mine], auxall.at[h, me, amine], "start")

    def forwards(h, zz, yy, op):
        u = zz * 2 + yy
        xs, xas = xall.at[h, u, mine], auxall.at[h, u, amine]

        @pl.when(yy == y)
        def _():
            @pl.when(jnp.logical_and(zz < z, z < 3))
            def _():
                link_send(h, u, xs, xas, 0, up, op)

            @pl.when(jnp.logical_and(zz > z, z > 0))
            def _():
                link_send(h, u, xs, xas, 1, down, op)

            link_send(h, u, xs, xas, 2, ynbr, op)

        d2d_send(h, u, op)

    def piece(k):
        along_z = (1 - k % 2) * (1 - k // 6)
        i = k // 2
        first = 1 - (i + 2) // 3
        zi = _z_order(z, i - i // 3)
        zy = first * z + (1 - first) * _z_order(z, (i - 1) * (1 - first))
        zz = along_z * zi + (1 - along_z) * zy
        yy = along_z * y + (1 - along_z) * (1 - y)
        return zz, yy

    def ag_step(h, k):
        zz, yy = piece(k)
        u = zz * 2 + yy
        rcopy(auxall.at[h, u, amine], auxall.at[h, u, amine], sasem.at[h, u, 0], lasem.at[h, u], partner).wait_recv()
        rcopy(xall.at[h, u, mine], xall.at[h, u, mine], ssem.at[h, u, 0], lsem.at[h, u], partner).wait_recv()
        forwards(h, zz, yy, "start")

    def d2d_wait(h, k):
        zz, yy = piece(k)
        u = zz * 2 + yy
        oth = pl.ds(oth0, HALF)
        aoth = pl.ds(pl.multiple_of((1 - c) * 8, 8), 8)
        rcopy(auxall.at[h, u, aoth], auxall.at[h, u, aoth], sasem.at[h, u, 0], dasem.at[h, u], partner).wait_recv()
        rcopy(xall.at[h, u, oth], xall.at[h, u, oth], ssem.at[h, u, 0], dsem.at[h, u], partner).wait_recv()
        return u

    lane = lax.broadcasted_iota(jnp.int32, (T, 4 * EL * CAP), 1)
    sub = lax.broadcasted_iota(jnp.int32, (T, 4 * EL * CAP), 0)
    spread[...] = jnp.where(lane // CAP == sub, 1.0, 0.0).astype(BF16)

    def gather(h, u):
        aux = auxall[h, u]
        eg = (lax.broadcasted_iota(jnp.int32, (EL, T), 0) + z * EL).astype(F32)
        hit = jnp.zeros((EL, T), F32)
        gate = jnp.zeros((EL, T), F32)
        for j in range(TOP):
            eq = aux[j:j + 1, :] == eg
            hit = jnp.where(eq, 1.0, hit)
            gate = jnp.where(eq, aux[TOP + j:TOP + j + 1, :], gate)
        before = lax.broadcasted_iota(jnp.int32, (T, T), 0) < lax.broadcasted_iota(jnp.int32, (T, T), 1)
        tri = jnp.where(before, 1.0, 0.0).astype(BF16)
        slot = jnp.dot(hit.astype(BF16), tri, preferred_element_type=F32)
        keep = jnp.logical_and(hit > 0.5, slot < CAP - 0.5)
        slot = jnp.where(keep, slot, -1.0)
        g1 = gate.astype(BF16).astype(F32)
        r1 = gate - g1
        g2 = r1.astype(BF16).astype(F32)
        g3 = r1 - g2
        stack = jnp.concatenate([slot, g1, g2, g3, jnp.zeros((T - 4 * EL, T), F32)], axis=0)
        tab[h, u] = stack.T.astype(BF16)
        pos = lax.broadcasted_iota(jnp.int32, (EL, CAP, T), 1).astype(F32)
        hot = jnp.where(slot[:, None, :] == pos, 1.0, 0.0).reshape(EL * CAP, T).astype(BF16)
        rows = pl.ds(pl.multiple_of(u * CAP, CAP), CAP)
        for n in range(0, d, 512):
            xg = jnp.dot(hot, xall[h, u, :, n:n + 512], preferred_element_type=F32).astype(BF16)
            xe[:, rows, n:n + 512] = xg.reshape(EL, CAP, 512)

    def expert(q):
        e, s = q % EL, q % NS
        c1, c3, c2 = wcopies(q)
        c1.wait()
        a = jnp.dot(xe[e], w1b[s], preferred_element_type=F32)
        c3.wait()
        b = jnp.dot(xe[e], w3b[s], preferred_element_type=F32)
        hh = (a * jax.nn.sigmoid(a) * b).astype(BF16)
        c2.wait()
        for n in range(0, d, 512):
            xe[e, :, n:n + 512] = jnp.dot(hh, w2b[s, :, n:n + 512], preferred_element_type=F32).astype(BF16)

        @pl.when(q + NS < 2 * EL)
        def _():
            for cp in wcopies(q + NS):
                cp.start()

    slots_of = (lax.broadcasted_iota(jnp.int32, (T, EL * CAP), 1) % CAP).astype(F32)

    def dcopy(h, u):
        return rcopy(dstage.at[u], drecv.at[h, u], rd_s.at[h, u], rd_r.at[h, u], partner)

    def ycopy(h, zz):
        return rcopy(ystage.at[zz], yrecv.at[h, zz], ry_s.at[h, zz], ry_r.at[h, zz], ynbr)

    def zcopy(h, zz, slot, dev):
        return rcopy(zstage.at[zz], zrecv.at[h, slot], rz_s.at[h, zz], rz_r.at[h, slot], dev)

    def fcopy():
        return rcopy(fstage, frecv, rf_s, rf_r, partner)

    def combine(h, u):
        tb = jnp.concatenate([tab[h, u, mine], tab[h, u, pl.ds(oth0, HALF)]], axis=0)
        ex = jnp.dot(tb, spread[...], preferred_element_type=F32)
        n0 = EL * CAP
        on = ex[:, :n0] == slots_of
        lhs = jnp.concatenate([jnp.where(on, ex[:, k * n0:(k + 1) * n0], 0.0).astype(BF16) for k in (1, 2, 3)], axis=0)
        rows = pl.ds(pl.multiple_of(u * CAP, CAP), CAP)
        if h == 1:
            dcopy(0, u).wait_send()
        for n in range(0, d, 512):
            yy = xe[:, rows, n:n + 512].reshape(EL * CAP, 512)
            p3 = jnp.dot(lhs, yy, preferred_element_type=F32)
            p = p3[:T] + p3[T:2 * T] + p3[2 * T:]
            pown[u, :, n:n + 512] = p[:HALF]
            dstage[u, :, n:n + 512] = p[HALF:].astype(BF16)
        dcopy(h, u).start()

    def fin_y(h, i):
        zz = _r_order(z, i)
        u = zz * 2 + (1 - y)
        dcopy(h, u).wait_recv()
        if h == 1:
            ycopy(0, zz).wait_send()
        ystage[zz] = (pown[u] + drecv[h, u].astype(F32)).astype(BF16)
        ycopy(h, zz).start()

    def fin_z(h, i):
        zz = _r_order(z, i)
        u = zz * 2 + y
        dcopy(h, u).wait_recv()
        ycopy(h, zz).wait_recv()

        @pl.when(jnp.logical_or(jnp.logical_and(zz > z, z > 0), jnp.logical_and(zz < z, z < 3)))
        def _():
            zcopy(h, zz, zz, up).wait_recv()
            pown[u] = pown[u] + zrecv[h, zz].astype(F32)

        if h == 1:
            zcopy(0, zz, zz, up).wait_send()
        zstage[zz] = (pown[u] + drecv[h, u].astype(F32) + yrecv[h, zz].astype(F32)).astype(BF16)

        @pl.when(zz == z + 1)
        def _():
            zcopy(h, zz, 4, up).start()

        @pl.when(zz > z + 1)
        def _():
            zcopy(h, zz, zz, up).start()

        @pl.when(zz < z)
        def _():
            zcopy(h, zz, zz, down).start()

    def fin_own(h):
        u = me
        dcopy(h, u).wait_recv()
        ycopy(h, z).wait_recv()
        pown[u] = pown[u] + drecv[h, u].astype(F32) + yrecv[h, z].astype(F32)

        @pl.when(z < 3)
        def _():
            zcopy(h, z, z, up).wait_recv()
            pown[u] = pown[u] + zrecv[h, z].astype(F32)

        @pl.when(z > 0)
        def _():
            zcopy(h, z, 4, up).wait_recv()
            pown[u] = pown[u] + zrecv[h, 4].astype(F32)

        @pl.when(c == h)
        def _():
            out_ref[mine, :] = pown[u].astype(BF16)

        @pl.when(c != h)
        def _():
            fstage[...] = pown[u].astype(BF16)
            fcopy().start()

    for h in range(2):
        @pl.when(c == h)
        def _():
            own_full(h, "start")
    own_start(0)
    gather(0, me)

    def a_body(k, _):
        @pl.when(k < 7)
        def _():
            ag_step(0, k)

        @pl.when(k == 4)
        def _():
            own_start(1)

        @pl.when(k > 0)
        def _():
            gather(0, d2d_wait(0, k - 1))
        return 0

    lax.fori_loop(0, 8, a_body, 0)

    def ffn_a(e, _):
        expert(e)
        for k, at in enumerate((4, 5, 9, 10, 14, 15)):
            @pl.when(e == at)
            def _():
                ag_step(1, k)
        return 0

    lax.fori_loop(0, EL, ffn_a, 0)

    def comb_all(h):
        def body(i, _):
            yy = (1 - i // 4) * (1 - y) + (i // 4) * y
            combine(h, _r_order(z, i % 4) * 2 + yy)

            @pl.when(jnp.logical_and(i > 0, i < 5))
            def _():
                fin_y(h, i - 1)
            if h == 0:
                @pl.when(i == 3)
                def _():
                    ag_step(1, 6)
            return 0
        lax.fori_loop(0, 8, body, 0)

    comb_all(0)

    def b_body(k, _):
        @pl.when(k == 0)
        def _():
            gather(1, me)

        @pl.when(k > 0)
        def _():
            gather(1, d2d_wait(1, k - 1))
        return 0

    lax.fori_loop(0, 8, b_body, 0)

    def ffn_b(e, _):
        expert(EL + e)
        for i in range(3):
            @pl.when(e == 4 * i + 1 + 4 * inner)
            def _():
                fin_z(0, i)
        return 0

    lax.fori_loop(0, EL, ffn_b, 0)
    fin_own(0)
    comb_all(1)

    def last_z(i, _):
        fin_z(1, i)
        return 0

    lax.fori_loop(0, 3, last_z, 0)
    fin_own(1)

    fcopy().wait_recv()
    out_ref[pl.ds(oth0, HALF), :] = frecv[...]

    fcopy().wait_send()
    for h in range(2):
        @pl.when(c == h)
        def _():
            own_full(h, "send")
        own_links(h, xall.at[h, me, mine], auxall.at[h, me, amine], "send")

        def drain(k, _):
            zz, yy = piece(k)
            forwards(h, zz, yy, "send")
            return 0
        lax.fori_loop(0, 7, drain, 0)

    def drain_r(i, _):
        zz = _r_order(z, i)
        dcopy(1, zz * 2).wait_send()
        dcopy(1, zz * 2 + 1).wait_send()
        ycopy(1, zz).wait_send()

        @pl.when(i < 3)
        def _():
            zcopy(1, zz, zz, up).wait_send()
        return 0
    lax.fori_loop(0, 4, drain_r, 0)


def solution(mesh):
    rows = P(("dp", "ep", "tp"), None)

    def local(x, idx, g, w1, w3, w2):
        d = x.shape[1]
        f = w1.shape[2]
        aux = jnp.concatenate([idx.T.astype(F32), g.T], axis=0)
        vm = pl.BlockSpec(memory_space=pltpu.VMEM)
        hbm = pl.BlockSpec(memory_space=pl.ANY)
        dma = pltpu.SemaphoreType.DMA
        return pl.pallas_call(
            _kernel,
            out_shape=jax.ShapeDtypeStruct((T, d), BF16),
            in_specs=[vm, vm, hbm, hbm, hbm],
            out_specs=vm,
            scratch_shapes=[
                pltpu.VMEM((2, UNITS, T, d), BF16),
                pltpu.VMEM((2, UNITS, 2 * TOP, T), F32),
                pltpu.VMEM((EL, ROWS, d), BF16),
                pltpu.VMEM((NS, d, f), BF16),
                pltpu.VMEM((NS, d, f), BF16),
                pltpu.VMEM((NS, f, d), BF16),
                pltpu.VMEM((T, 4 * EL * CAP), BF16),
                pltpu.VMEM((2, UNITS, T, T), BF16),
                pltpu.VMEM((UNITS, HALF, d), F32),
                pltpu.VMEM((UNITS, HALF, d), BF16),
                pltpu.VMEM((2, UNITS, HALF, d), BF16),
                pltpu.VMEM((4, HALF, d), BF16),
                pltpu.VMEM((2, 4, HALF, d), BF16),
                pltpu.VMEM((4, HALF, d), BF16),
                pltpu.VMEM((2, 5, HALF, d), BF16),
                pltpu.VMEM((HALF, d), BF16),
                pltpu.VMEM((HALF, d), BF16),
                dma((2, UNITS)), dma((2, UNITS)), dma((2, UNITS)), dma((2, UNITS)),
                dma((2, UNITS, 4)), dma((2, UNITS, 4)),
                dma((NS, 3)),
                dma((2, UNITS)), dma((2, UNITS)),
                dma((2, 4)), dma((2, 4)),
                dma((2, 4)), dma((2, 5)),
                dma, dma,
            ],
            compiler_params=pltpu.CompilerParams(collective_id=0, has_side_effects=True,
                                                 vmem_limit_bytes=67043328),
        )(x, aux, w1, w3, w2)

    return jax.shard_map(local, mesh=mesh,
                         in_specs=(rows, rows, rows, P("ep", None, "tp"), P("ep", None, "tp"), P("ep", "tp", None)),
                         out_specs=rows, check_vma=False)
```

time: 1170 us -> 161 us (0.14)
  blocking collectives: 573 us -> 0 us
  waiting for transfers between devices: 384 us -> 0 us
  Pallas kernels: 0 us -> 157 us
  local copies, waits for them, and re-layouts: 81.1 us -> 1.88 us
  matrix products: 67.9 us -> 0 us
  other arithmetic: 43.3 us -> 1.97 us
  between operations: 13.5 us -> 0.01 us
    all_to_all x2 -> x0, blocking collectives: 573 us -> none  [the longest x1 381 us: local(): parts = lax.all_to_all(yp, 'tp', 0, 0, tiled=True)]
    all_gather x1 -> x0, waiting for transfers between devices: 201 us -> none  [local(): allr = lax.all_gather(recv, 'tp', axis=0)]
    all_to_all x1 -> x0, waiting for transfers between devices: 182 us -> none  [local(): back = lax.all_to_all(y, 'ep', 0, 0, tiled=True).reshape(n_exp * cap, d)]
    pallas_call x0 -> x1, Pallas kernels: none -> 157 us  [local(): pl.pallas_call(_kernel, out_shape=jax.ShapeDtypeStruct((T, d), BF16), in_...]
    dot_general x3 -> x0, matrix products: 67.9 us -> none  [the longest x1 23.7 us: local(): h3 = jnp.einsum('erd,edf->erf', xe, w3, preferred_element_type=jnp.float32)]
    reduce_sum x3 -> x0, other arithmetic: 23.8 us -> none  [the longest x1 16.4 us: local(): y = jnp.sum(parts.astype(jnp.float32), axis=0).astype(jnp.bfloat16)]
    reshape x1 -> x0, local copies, waits for them, and re-layouts: 23 us -> none  [local(): yp = yp.reshape(el, tp, ep, cap, d).transpose(1, 2, 0, 3, 4)]
    all_gather x1 -> x0, local copies, waits for them, and re-layouts: 22.9 us -> none  [local(): allr = lax.all_gather(recv, 'tp', axis=0)]
  transfers between devices with their start and end apart: 2 -> 0, of which waited for: 2 -> 0; matrix products, arithmetic and copies ran while one was open for 0% -> 0% of each run, Pallas kernels for 0% -> 0%
where the time goes in v1:
time: 161 us
  Pallas kernels  157 us (98%)
  other arithmetic  1.97 us (1%)
  local copies, waits for them, and re-layouts  1.88 us (1%)
    pallas_call x1, Pallas kernels, local(): pl.pallas_call(_kernel, out_shape=jax.ShapeDtypeStruct((T, d), BF16), in_...  157 us

profile of v1, /device:TPU:0, one launch (start us, length us, event | category | flops | bytes accessed | tf_op | source)
XLA Modules:
  0.0 160.6 jit_solution(6436528663331137568)
XLA Ops:
  0.0 0.7 convert_bitcast_fusion
  0.7 1.3 pad_maximum_fusion.aux_ref
  2.0 156.8 %shard_map.64 = bf16[128,2048]{1,0:T(8,128)(2,1)} custom-call(bf16[128,2048]{1,0:T(8,128)(2,1)} %x_ref.1, f32[16,128]{1,0:T(8,128)} %pad_maximum_fusion.aux_ref, bf16[16,2048,256]{2,1,0:T(8,128)(2,1)} %w1_ref.1, bf16[16,2048,256]{2,1,0:T(8,128)(2,1)} %w3_ref.1, bf16[16,256,2048]{2,1,0:T(8,128)(2,1)} %w2_ref.1), custom_call_target="tpu_custom_call" | custom-call | tf_op jit(solution)/shard_map/pallas_call | solution.py:446
  158.7 1.9 %copy.8 = bf16[128,2048]{1,0:T(8,128)(2,1)} copy(bf16[128,2048]{1,0:T(8,128)(2,1)} %shard_map.64) | data formatting | bytes 1048576

commit v2 on v1

--- a/solution.py
+++ b/solution.py
@@ -218,11 +218,11 @@
         e, s = q % EL, q % NS
         c1, c3, c2 = wcopies(q)
         c1.wait()
+        c3.wait()
+        c2.wait()
         a = jnp.dot(xe[e], w1b[s], preferred_element_type=F32)
-        c3.wait()
         b = jnp.dot(xe[e], w3b[s], preferred_element_type=F32)
         hh = (a * jax.nn.sigmoid(a) * b).astype(BF16)
-        c2.wait()
         for n in range(0, d, 512):
             xe[e, :, n:n + 512] = jnp.dot(hh, w2b[s, :, n:n + 512], preferred_element_type=F32).astype(BF16)
 

time: 161 us -> 142 us (0.88)
  the two profiles are of different devices: /device:TPU:0 before, /device:TPU:11 now
where the time goes in v2:
time: 142 us
  Pallas kernels  138 us (97%)
  other arithmetic  1.97 us (1%)
  local copies, waits for them, and re-layouts  1.88 us (1%)
    pallas_call x1, Pallas kernels, local(): pl.pallas_call(_kernel, out_shape=jax.ShapeDtypeStruct((T, d), BF16), in_...  138 us

profile of v2, /device:TPU:11, one launch (start us, length us, event | category | flops | bytes accessed | tf_op | source)
XLA Modules:
  0.0 142.2 jit_solution(4698896858348790300)
XLA Ops:
  0.0 0.7 convert_bitcast_fusion
  0.7 1.3 pad_maximum_fusion.aux_ref
  2.0 138.4 %shard_map.64 = bf16[128,2048]{1,0:T(8,128)(2,1)} custom-call(bf16[128,2048]{1,0:T(8,128)(2,1)} %x_ref.1, f32[16,128]{1,0:T(8,128)} %pad_maximum_fusion.aux_ref, bf16[16,2048,256]{2,1,0:T(8,128)(2,1)} %w1_ref.1, bf16[16,2048,256]{2,1,0:T(8,128)(2,1)} %w3_ref.1, bf16[16,256,2048]{2,1,0:T(8,128)(2,1)} %w2_ref.1), custom_call_target="tpu_custom_call" | custom-call | tf_op jit(solution)/shard_map/pallas_call | solution.py:446
  140.4 1.9 %copy.8 = bf16[128,2048]{1,0:T(8,128)(2,1)} copy(bf16[128,2048]{1,0:T(8,128)(2,1)} %shard_map.64) | data formatting | bytes 1048576

commit v3 on v2

--- a/solution.py
+++ b/solution.py
@@ -13,6 +13,7 @@
 
 T = 128
 HALF = T // 2
+PART = HALF // 2
 TOP = 8
 EL = 16
 CAP = 32
@@ -38,14 +39,15 @@
 
 def _kernel(x_ref, aux_ref, w1_ref, w3_ref, w2_ref, out_ref,
             xall, auxall, xe, w1b, w3b, w2b, spread, tab, pown, dstage, drecv, ystage, yrecv, zstage, zrecv,
-            fstage, frecv,
-            lsem, lasem, dsem, dasem, ssem, sasem, wsem, rd_s, rd_r, ry_s, ry_r, rz_s, rz_r, rf_s, rf_r):
+            fstage, frecv, astage, arecv,
+            lsem, lasem, dsem, dasem, ssem, sasem, wsem, rd_s, rd_r, ry_s, ry_r, rz_s, rz_r, ra_s, ra_r, rf_s, rf_r):
     d = x_ref.shape[1]
     z = lax.axis_index("ep")
     tp = lax.axis_index("tp")
     y = tp // 2
     c = tp % 2
     me = z * 2 + y
+    pz = z + 1 - 2 * (z % 2)
     row0 = pl.multiple_of(c * HALF, HALF)
     oth0 = pl.multiple_of((1 - c) * HALF, HALF)
     mine = pl.ds(row0, HALF)
@@ -83,79 +85,96 @@
     inner = (z + 1) // 2 - 2 * (z // 3)
     pl.semaphore_wait(bar, 3 + inner)
 
-    def link_send(h, u, xs, xas, k, dev, op):
-        cx = rcopy(xs, xall.at[h, u, mine], ssem.at[h, u, k], lsem.at[h, u], dev)
-        ca = rcopy(xas, auxall.at[h, u, amine], sasem.at[h, u, k], lasem.at[h, u], dev)
-        if op == "start":
-            ca.start()
-            cx.start()
-        else:
-            ca.wait_send()
-            cx.wait_send()
-
-    def d2d_send(h, u, op):
-        cx = rcopy(xall.at[h, u, mine], xall.at[h, u, mine], ssem.at[h, u, 3], dsem.at[h, u], partner)
-        ca = rcopy(auxall.at[h, u, amine], auxall.at[h, u, amine], sasem.at[h, u, 3], dasem.at[h, u], partner)
-        if op == "start":
-            ca.start()
-            cx.start()
-        else:
-            ca.wait_send()
-            cx.wait_send()
+    def part(r0, p):
+        return pl.ds(pl.multiple_of(r0 + p * PART, PART), PART)
+
+    def link_send(h, u, p, k, dev, op, xs=None, xas=None):
+        xs = xall.at[h, u, part(row0, p)] if xs is None else xs
+        cx = rcopy(xs, xall.at[h, u, part(row0, p)], ssem.at[h, u, p, k], lsem.at[h, u, p], dev)
+        if p == 0:
+            xas = auxall.at[h, u, amine] if xas is None else xas
+            ca = rcopy(xas, auxall.at[h, u, amine], sasem.at[h, u, k], lasem.at[h, u], dev)
+            ca.start() if op == "start" else ca.wait_send()
+        cx.start() if op == "start" else cx.wait_send()
+
+    def d2d_send(h, u, p, op):
+        cx = rcopy(xall.at[h, u, part(row0, p)], xall.at[h, u, part(row0, p)], ssem.at[h, u, p, 3],
+                   dsem.at[h, u, p], partner)
+        if p == 0:
+            ca = rcopy(auxall.at[h, u, amine], auxall.at[h, u, amine], sasem.at[h, u, 3], dasem.at[h, u], partner)
+            ca.start() if op == "start" else ca.wait_send()
+        cx.start() if op == "start" else cx.wait_send()
 
     def own_full(h, op):
-        cx = rcopy(x_ref, xall.at[h, me], ssem.at[h, me, 3], dsem.at[h, me], partner)
+        cx = rcopy(x_ref, xall.at[h, me], ssem.at[h, me, 0, 3], dsem.at[h, me, 0], partner)
         ca = rcopy(aux_ref, auxall.at[h, me], sasem.at[h, me, 3], dasem.at[h, me], partner)
-        if op == "start":
-            ca.start()
-            cx.start()
-        elif op == "send":
-            ca.wait_send()
-            cx.wait_send()
-        else:
-            ca.wait_recv()
-            cx.wait_recv()
-
-    def own_links(h, xs, xas, op):
-        @pl.when(z < 3)
-        def _():
-            link_send(h, me, xs, xas, 0, up, op)
-
-        @pl.when(z > 0)
-        def _():
-            link_send(h, me, xs, xas, 1, down, op)
-
-        link_send(h, me, xs, xas, 2, ynbr, op)
+        for cp in (ca, cx):
+            if op == "start":
+                cp.start()
+            elif op == "send":
+                cp.wait_send()
+            else:
+                cp.wait_recv()
+
+    def own_links(h, op, from_input):
+        for p in range(2):
+            xs = x_ref.at[part(row0, p)] if from_input else None
+            xas = aux_ref.at[amine] if from_input else None
+
+            @pl.when(z < 3)
+            def _():
+                link_send(h, me, p, 0, up, op, xs, xas)
+
+            @pl.when(z > 0)
+            def _():
+                link_send(h, me, p, 1, down, op, xs, xas)
+
+            link_send(h, me, p, 2, ynbr, op, xs, xas)
 
     def own_start(h):
         @pl.when(c == h)
         def _():
-            own_links(h, x_ref.at[mine], aux_ref.at[amine], "start")
+            own_links(h, "start", True)
             xall[h, me] = x_ref[...]
             auxall[h, me] = aux_ref[...]
 
         @pl.when(c != h)
         def _():
             own_full(h, "recv")
-            own_links(h, xall.at[h, me, mine], auxall.at[h, me, amine], "start")
-
-    def forwards(h, zz, yy, op):
+            own_links(h, "start", False)
+
+    def forwards(h, zz, yy, p, op):
         u = zz * 2 + yy
-        xs, xas = xall.at[h, u, mine], auxall.at[h, u, amine]
 
         @pl.when(yy == y)
         def _():
             @pl.when(jnp.logical_and(zz < z, z < 3))
             def _():
-                link_send(h, u, xs, xas, 0, up, op)
+                link_send(h, u, p, 0, up, op)
 
             @pl.when(jnp.logical_and(zz > z, z > 0))
             def _():
-                link_send(h, u, xs, xas, 1, down, op)
-
-            link_send(h, u, xs, xas, 2, ynbr, op)
-
-        d2d_send(h, u, op)
+                link_send(h, u, p, 1, down, op)
+
+            if p == 0:
+                link_send(h, u, p, 2, ynbr, op)
+            else:
+                @pl.when(zz != pz)
+                def _():
+                    link_send(h, u, p, 2, ynbr, op)
+
+        d2d_send(h, u, p, op)
+
+    def alt_forward(h, op):
+        u = z * 2 + (1 - y)
+
+        @pl.when(z % 2 == 0)
+        def _():
+            link_send(h, u, 1, 0, up, op)
+
+        @pl.when(z % 2 == 1)
+        def _():
+            link_send(h, u, 1, 1, down, op)
 
     def piece(k):
         along_z = (1 - k % 2) * (1 - k // 6)
@@ -167,25 +186,25 @@
         yy = along_z * y + (1 - along_z) * (1 - y)
         return zz, yy
 
-    def ag_step(h, k):
+    def ag_sub(h, k, p):
         zz, yy = piece(k)
         u = zz * 2 + yy
-        rcopy(auxall.at[h, u, amine], auxall.at[h, u, amine], sasem.at[h, u, 0], lasem.at[h, u], partner).wait_recv()
-        rcopy(xall.at[h, u, mine], xall.at[h, u, mine], ssem.at[h, u, 0], lsem.at[h, u], partner).wait_recv()
-        forwards(h, zz, yy, "start")
+        if p == 0:
+            rcopy(auxall.at[h, u, amine], auxall.at[h, u, amine], sasem.at[h, u, 0], lasem.at[h, u],
+                  partner).wait_recv()
+        rcopy(xall.at[h, u, part(row0, p)], xall.at[h, u, part(row0, p)], ssem.at[h, u, p, 0], lsem.at[h, u, p],
+              partner).wait_recv()
+        forwards(h, zz, yy, p, "start")
 
     def d2d_wait(h, k):
         zz, yy = piece(k)
         u = zz * 2 + yy
-        oth = pl.ds(oth0, HALF)
         aoth = pl.ds(pl.multiple_of((1 - c) * 8, 8), 8)
         rcopy(auxall.at[h, u, aoth], auxall.at[h, u, aoth], sasem.at[h, u, 0], dasem.at[h, u], partner).wait_recv()
-        rcopy(xall.at[h, u, oth], xall.at[h, u, oth], ssem.at[h, u, 0], dsem.at[h, u], partner).wait_recv()
+        for p in range(2):
+            rcopy(xall.at[h, u, part(oth0, p)], xall.at[h, u, part(oth0, p)], ssem.at[h, u, p, 0], dsem.at[h, u, p],
+                  partner).wait_recv()
         return u
-
-    lane = lax.broadcasted_iota(jnp.int32, (T, 4 * EL * CAP), 1)
-    sub = lax.broadcasted_iota(jnp.int32, (T, 4 * EL * CAP), 0)
-    spread[...] = jnp.where(lane // CAP == sub, 1.0, 0.0).astype(BF16)
 
     def gather(h, u):
         aux = auxall[h, u]
@@ -236,11 +255,17 @@
     def dcopy(h, u):
         return rcopy(dstage.at[u], drecv.at[h, u], rd_s.at[h, u], rd_r.at[h, u], partner)
 
-    def ycopy(h, zz):
-        return rcopy(ystage.at[zz], yrecv.at[h, zz], ry_s.at[h, zz], ry_r.at[h, zz], ynbr)
-
-    def zcopy(h, zz, slot, dev):
-        return rcopy(zstage.at[zz], zrecv.at[h, slot], rz_s.at[h, zz], rz_r.at[h, slot], dev)
+    def sub(p):
+        return pl.ds(p * PART, PART)
+
+    def ycopy(h, zz, p):
+        return rcopy(ystage.at[zz, sub(p)], yrecv.at[h, zz, sub(p)], ry_s.at[h, zz, p], ry_r.at[h, zz, p], ynbr)
+
+    def zcopy(h, zz, slot, p, dev):
+        return rcopy(zstage.at[zz, sub(p)], zrecv.at[h, slot, sub(p)], rz_s.at[h, zz, p], rz_r.at[h, slot, p], dev)
+
+    def acopy(h, dev):
+        return rcopy(astage.at[h], arecv.at[h], ra_s.at[h], ra_r.at[h], dev)
 
     def fcopy():
         return rcopy(fstage, frecv, rf_s, rf_r, partner)
@@ -262,57 +287,98 @@
             dstage[u, :, n:n + 512] = p[HALF:].astype(BF16)
         dcopy(h, u).start()
 
+    def alt_send(h):
+        u = pz * 2 + (1 - y)
+        dcopy(h, u).wait_recv()
+        astage[h] = (pown[u, PART:, :] + drecv[h, u, PART:, :].astype(F32)).astype(BF16)
+
+        @pl.when(z % 2 == 0)
+        def _():
+            acopy(h, up).start()
+
+        @pl.when(z % 2 == 1)
+        def _():
+            acopy(h, down).start()
+
     def fin_y(h, i):
         zz = _r_order(z, i)
         u = zz * 2 + (1 - y)
-        dcopy(h, u).wait_recv()
+
+        @pl.when(zz != pz)
+        def _():
+            dcopy(h, u).wait_recv()
+
         if h == 1:
-            ycopy(0, zz).wait_send()
-        ystage[zz] = (pown[u] + drecv[h, u].astype(F32)).astype(BF16)
-        ycopy(h, zz).start()
+            ycopy(0, zz, 0).wait_send()
+        ystage[zz, :PART, :] = (pown[u, :PART, :] + drecv[h, u, :PART, :].astype(F32)).astype(BF16)
+        ycopy(h, zz, 0).start()
+
+        @pl.when(zz == z)
+        def _():
+            acopy(h, up).wait_recv()
+            pown[u, PART:, :] = pown[u, PART:, :] + arecv[h].astype(F32)
+
+        @pl.when(zz != pz)
+        def _():
+            if h == 1:
+                ycopy(0, zz, 1).wait_send()
+            ystage[zz, PART:, :] = (pown[u, PART:, :] + drecv[h, u, PART:, :].astype(F32)).astype(BF16)
+            ycopy(h, zz, 1).start()
 
     def fin_z(h, i):
         zz = _r_order(z, i)
         u = zz * 2 + y
         dcopy(h, u).wait_recv()
-        ycopy(h, zz).wait_recv()
-
-        @pl.when(jnp.logical_or(jnp.logical_and(zz > z, z > 0), jnp.logical_and(zz < z, z < 3)))
-        def _():
-            zcopy(h, zz, zz, up).wait_recv()
-            pown[u] = pown[u] + zrecv[h, zz].astype(F32)
-
-        if h == 1:
-            zcopy(0, zz, zz, up).wait_send()
-        zstage[zz] = (pown[u] + drecv[h, u].astype(F32) + yrecv[h, zz].astype(F32)).astype(BF16)
-
-        @pl.when(zz == z + 1)
-        def _():
-            zcopy(h, zz, 4, up).start()
-
-        @pl.when(zz > z + 1)
-        def _():
-            zcopy(h, zz, zz, up).start()
-
-        @pl.when(zz < z)
-        def _():
-            zcopy(h, zz, zz, down).start()
+        for p in range(2):
+            r = slice(p * PART, (p + 1) * PART)
+
+            def add_y():
+                ycopy(h, zz, p).wait_recv()
+                pown[u, r, :] = pown[u, r, :] + yrecv[h, zz, r, :].astype(F32)
+
+            if p == 0:
+                add_y()
+            else:
+                pl.when(zz != pz)(add_y)
+
+            @pl.when(jnp.logical_or(jnp.logical_and(zz > z, z > 0), jnp.logical_and(zz < z, z < 3)))
+            def _():
+                zcopy(h, zz, zz, p, up).wait_recv()
+                pown[u, r, :] = pown[u, r, :] + zrecv[h, zz, r, :].astype(F32)
+
+            if h == 1:
+                zcopy(0, zz, zz, p, up).wait_send()
+            zstage[zz, r, :] = (pown[u, r, :] + drecv[h, u, r, :].astype(F32)).astype(BF16)
+
+            @pl.when(zz == z + 1)
+            def _():
+                zcopy(h, zz, 4, p, up).start()
+
+            @pl.when(zz > z + 1)
+            def _():
+                zcopy(h, zz, zz, p, up).start()
+
+            @pl.when(zz < z)
+            def _():
+                zcopy(h, zz, zz, p, down).start()
 
     def fin_own(h):
         u = me
         dcopy(h, u).wait_recv()
-        ycopy(h, z).wait_recv()
-        pown[u] = pown[u] + drecv[h, u].astype(F32) + yrecv[h, z].astype(F32)
-
-        @pl.when(z < 3)
-        def _():
-            zcopy(h, z, z, up).wait_recv()
-            pown[u] = pown[u] + zrecv[h, z].astype(F32)
-
-        @pl.when(z > 0)
-        def _():
-            zcopy(h, z, 4, up).wait_recv()
-            pown[u] = pown[u] + zrecv[h, 4].astype(F32)
+        for p in range(2):
+            r = slice(p * PART, (p + 1) * PART)
+            ycopy(h, z, p).wait_recv()
+            pown[u, r, :] = pown[u, r, :] + drecv[h, u, r, :].astype(F32) + yrecv[h, z, r, :].astype(F32)
+
+            @pl.when(z < 3)
+            def _():
+                zcopy(h, z, z, p, up).wait_recv()
+                pown[u, r, :] = pown[u, r, :] + zrecv[h, z, r, :].astype(F32)
+
+            @pl.when(z > 0)
+            def _():
+                zcopy(h, z, 4, p, up).wait_recv()
+                pown[u, r, :] = pown[u, r, :] + zrecv[h, 4, r, :].astype(F32)
 
         @pl.when(c == h)
         def _():
@@ -328,30 +394,55 @@
         def _():
             own_full(h, "start")
     own_start(0)
+    lane = lax.broadcasted_iota(jnp.int32, (T, 4 * EL * CAP), 1)
+    row_id = lax.broadcasted_iota(jnp.int32, (T, 4 * EL * CAP), 0)
+    spread[...] = jnp.where(lane // CAP == row_id, 1.0, 0.0).astype(BF16)
+
     gather(0, me)
 
-    def a_body(k, _):
-        @pl.when(k < 7)
-        def _():
-            ag_step(0, k)
-
-        @pl.when(k == 4)
-        def _():
+    outer = 1 - inner
+    steps = (((0, 0, 2), (1, 0, 2), (2, 0, 1)), ((0, 1, 2), (1, 1, 2), (2, 1, 1)),
+             ((2, 0, 0), (3, 0, 2), (4, 0, 1)), ((2, 1, 0), (4, 1, 1)),
+             ((4, 0, 0), (5, 0, 2)), ((4, 1, 0), (5, 1, 2)), ((6, 0, 2),), ((6, 1, 2), (3, 1, 2)))
+
+    def a_body(it, _):
+        for n, todo in enumerate(steps):
+            @pl.when(it == n)
+            def _():
+                for k, p, where in todo:
+                    def step():
+                        ag_sub(0, k, p)
+                    if where == 2:
+                        step()
+                    else:
+                        pl.when(inner == where)(step)
+
+        @pl.when(it == 3 + 2 * outer)
+        def _():
+            alt_forward(0, "start")
             own_start(1)
 
-        @pl.when(k > 0)
-        def _():
-            gather(0, d2d_wait(0, k - 1))
+        @pl.when(it > 1)
+        def _():
+            last, late = it // 8, it // 5 - it // 8
+            gather(0, d2d_wait(0, (1 - last) * (it - 2 + late) + last * 3))
         return 0
 
-    lax.fori_loop(0, 8, a_body, 0)
+    lax.fori_loop(0, 9, a_body, 0)
 
     def ffn_a(e, _):
         expert(e)
-        for k, at in enumerate((4, 5, 9, 10, 14, 15)):
-            @pl.when(e == at)
-            def _():
-                ag_step(1, k)
+        for k in range(6):
+            for p in range(2):
+                if (k, p) == (3, 1):
+                    continue
+                at = (5, 7)[p] + 4 * (k // 2) - (4 * inner if k in (2, 4) else 0)
+
+                @pl.when(e == at)
+                def _():
+                    ag_sub(1, k, p)
+                    if (k, p) == (4, 1):
+                        alt_forward(1, "start")
         return 0
 
     lax.fori_loop(0, EL, ffn_a, 0)
@@ -359,15 +450,26 @@
     def comb_all(h):
         def body(i, _):
             yy = (1 - i // 4) * (1 - y) + (i // 4) * y
-            combine(h, _r_order(z, i % 4) * 2 + yy)
-
-            @pl.when(jnp.logical_and(i > 0, i < 5))
-            def _():
-                fin_y(h, i - 1)
+            j = i % 4
+            j = j + (1 - inner) * (1 - i // 4) * ((j % 3 + 1) // 2) * (3 - 2 * j)
+            combine(h, _r_order(z, j) * 2 + yy)
+
+            @pl.when(i == 2)
+            def _():
+                alt_send(h)
+
+            @pl.when(jnp.logical_and(i > 0, i < 2))
+            def _():
+                fin_y(h, 0)
+
+            @pl.when(jnp.logical_and(i > 2, i < 6))
+            def _():
+                fin_y(h, i - 2)
             if h == 0:
-                @pl.when(i == 3)
-                def _():
-                    ag_step(1, 6)
+                for at, k, p in ((5, 6, 0), (6, 6, 1), (7, 3, 1)):
+                    @pl.when(i == at)
+                    def _():
+                        ag_sub(1, k, p)
             return 0
         lax.fori_loop(0, 8, body, 0)
 
@@ -387,14 +489,17 @@
 
     def ffn_b(e, _):
         expert(EL + e)
-        for i in range(3):
-            @pl.when(e == 4 * i + 1 + 4 * inner)
+        for i, at in enumerate((2, 4, 8)):
+            @pl.when(e == at)
             def _():
                 fin_z(0, i)
+
+        @pl.when(e == 14)
+        def _():
+            fin_own(0)
         return 0
 
     lax.fori_loop(0, EL, ffn_b, 0)
-    fin_own(0)
     comb_all(1)
 
     def last_z(i, _):
@@ -412,11 +517,14 @@
         @pl.when(c == h)
         def _():
             own_full(h, "send")
-        own_links(h, xall.at[h, me, mine], auxall.at[h, me, amine], "send")
+        own_links(h, "send", False)
+        alt_forward(h, "send")
+        acopy(h, up).wait_send()
 
         def drain(k, _):
             zz, yy = piece(k)
-            forwards(h, zz, yy, "send")
+            for p in range(2):
+                forwards(h, zz, yy, p, "send")
             return 0
         lax.fori_loop(0, 7, drain, 0)
 
@@ -424,11 +532,16 @@
         zz = _r_order(z, i)
         dcopy(1, zz * 2).wait_send()
         dcopy(1, zz * 2 + 1).wait_send()
-        ycopy(1, zz).wait_send()
+        ycopy(1, zz, 0).wait_send()
+
+        @pl.when(zz != pz)
+        def _():
+            ycopy(1, zz, 1).wait_send()
 
         @pl.when(i < 3)
         def _():
-            zcopy(1, zz, zz, up).wait_send()
+            zcopy(1, zz, zz, 0, up).wait_send()
+            zcopy(1, zz, zz, 1, up).wait_send()
         return 0
     lax.fori_loop(0, 4, drain_r, 0)
 
@@ -466,12 +579,15 @@
                 pltpu.VMEM((2, 5, HALF, d), BF16),
                 pltpu.VMEM((HALF, d), BF16),
                 pltpu.VMEM((HALF, d), BF16),
-                dma((2, UNITS)), dma((2, UNITS)), dma((2, UNITS)), dma((2, UNITS)),
-                dma((2, UNITS, 4)), dma((2, UNITS, 4)),
+                pltpu.VMEM((2, PART, d), BF16),
+                pltpu.VMEM((2, PART, d), BF16),
+                dma((2, UNITS, 2)), dma((2, UNITS)), dma((2, UNITS, 2)), dma((2, UNITS)),
+                dma((2, UNITS, 2, 4)), dma((2, UNITS, 4)),
                 dma((NS, 3)),
                 dma((2, UNITS)), dma((2, UNITS)),
-                dma((2, 4)), dma((2, 4)),
-                dma((2, 4)), dma((2, 5)),
+                dma((2, 4, 2)), dma((2, 4, 2)),
+                dma((2, 4, 2)), dma((2, 5, 2)),
+                dma((2,)), dma((2,)),
                 dma, dma,
             ],
             compiler_params=pltpu.CompilerParams(collective_id=0, has_side_effects=True,

time: 142 us -> 140 us (0.986)
  the two profiles are of different devices: /device:TPU:11 before, /device:TPU:0 now
where the time goes in v3:
time: 140 us; the launch traced here: 139 us
  Pallas kernels  135 us (96%)
  other arithmetic  1.97 us (1%)
  local copies, waits for them, and re-layouts  1.88 us (1%)
    pallas_call x1, Pallas kernels, local(): pl.pallas_call(_kernel, out_shape=jax.ShapeDtypeStruct((T, d), BF16), in_...  135 us

profile of v3, /device:TPU:0, one launch (start us, length us, event | category | flops | bytes accessed | tf_op | source)
XLA Modules:
  0.0 139.2 jit_solution(120881737880148799)
XLA Ops:
  0.0 0.7 convert_bitcast_fusion
  0.7 1.3 pad_maximum_fusion.aux_ref
  2.0 135.4 %shard_map.64 = bf16[128,2048]{1,0:T(8,128)(2,1)} custom-call(bf16[128,2048]{1,0:T(8,128)(2,1)} %x_ref.1, f32[16,128]{1,0:T(8,128)} %pad_maximum_fusion.aux_ref, bf16[16,2048,256]{2,1,0:T(8,128)(2,1)} %w1_ref.1, bf16[16,2048,256]{2,1,0:T(8,128)(2,1)} %w3_ref.1, bf16[16,256,2048]{2,1,0:T(8,128)(2,1)} %w2_ref.1), custom_call_target="tpu_custom_call" | custom-call | tf_op jit(solution)/shard_map/pallas_call | solution.py:559
  137.4 1.9 %copy.8 = bf16[128,2048]{1,0:T(8,128)(2,1)} copy(bf16[128,2048]{1,0:T(8,128)(2,1)} %shard_map.64) | data formatting | bytes 1048576
